TPU v7x, 128 devices: a whole 4x4x4 slice. The times are simulated.
128 devices in a mesh: rep: 4 (over z_hi, core), row: 4 (over x), col: 8 (over z_lo, y).
Axes of the slice: x: 4, y: 4, z: 4 (z_hi: 2, z_lo: 2; z = z_hi * 2 + z_lo), core: 2. Of those that a mesh axis runs over, the one named last changes fastest.
Arguments:
- grad_parts: bfloat16 [4, 16384, 6144], P('rep', ('row', 'col')), may hold values from -0.03125 to 0.03125, as said below
- statistic: float32 [6144, 6144], P('row', 'col'), may hold values from -150 to 150, as said below
Outputs:
- gram_matrix: float32 [6144, 6144], P('row', 'col')
- statistic_next: float32 [6144, 6144], P('row', 'col')
Inputs may be any that keep to these rules, and one draw needn't show every extreme that they name: Every entry of grad_parts has a magnitude between 2^-10 and 2^-5. statistic is symmetric and positive definite.
All inputs are finite; a program needn't handle non-finite values.
Results may differ from a plain program's by a relative error of at most 0.008.
Values may be sent and summed in bfloat16 or wider, within the bound.
A program may use at most 128 MiB of HBM per device.

v0:
```python
import jax
import jax.numpy as jnp
from jax import lax
from jax.sharding import PartitionSpec as P


def shards(grad_parts, statistic):
    own_part = grad_parts[0].astype(jnp.float32)
    summed = lax.psum_scatter(own_part.astype(jnp.bfloat16), "rep", scatter_dimension=0, tiled=True)
    rows_panel = lax.all_to_all(summed, "row", split_axis=1, concat_axis=0, tiled=True)
    cols_panel = lax.all_to_all(summed, "col", split_axis=1, concat_axis=0, tiled=True)
    row_count = lax.axis_size("row")
    col_count = lax.axis_size("col")
    quarter = summed.shape[0]
    right_whole = lax.all_gather(cols_panel, "row", axis=0, tiled=True)
    right_order = (
        right_whole.reshape(row_count, col_count, quarter, -1)
        .transpose(1, 0, 2, 3)
        .reshape(row_count * col_count * quarter, -1)
    )
    partial_tile = lax.dot_general(
        lax.all_gather(rows_panel, "col", axis=0, tiled=True),
        right_order,
        (((0,), (0,)), ((), ())),
        preferred_element_type=jnp.float32,
    )
    portion = lax.psum_scatter(partial_tile, "rep", scatter_dimension=0, tiled=True)
    gram_tile = lax.all_gather(portion, "rep", axis=0, tiled=True)
    return (gram_tile, 0.95 * statistic + 0.05 * gram_tile)


def solution(mesh):
    return jax.shard_map(
        shards,
        mesh=mesh,
        in_specs=(P("rep", ("row", "col"), None), P("row", "col")),
        out_specs=(P("row", "col"), P("row", "col")),
        check_vma=False,
    )
```

profile of v0, /device:TPU:1, one launch (start us, length us, event | category | flops | bytes accessed | tf_op | source)
XLA Modules:
  0.0 441.3 jit_solution(476243138658292207)
XLA Ops:
  7.2 0.0 reduce-scatter.7.cloned.1.call-start
  7.2 0.7 reduce-scatter.7.cloned.1.call-update
  7.9 0.0 all-gather.6.cloned.1.call-start
  7.9 71.7 %reduce-scatter.7.cloned.1.call-done = bf16[128,6144]{1,0:T(8,128)(2,1)} async-done(((bf16[512,6144]{1,0:T(8,128)(2,1)}), bf16[128,6144]{1,0:T(8,128)(2,1)}) %reduce-scatter.7.cloned.1.call-update) | async-done | bytes 1572880
  79.6 1.9 copy.14
  81.5 24.2 %all_to_all.38 = bf16[128,8,768]{0,2,1:T(8,128)(2,1)S(1)} all-to-all(bf16[128,8,768]{0,2,1:T(8,128)(2,1)S(1)} %bitcast.15), channel_id=1, replica_groups=mesh['rep'=4,'row'=4,'col'=8] {'col'}, dimensions={1} | all-to-all | bytes 3145728 | tf_op jit(solution)/shard_map/all_to_all | solution.py:11
  105.7 1.6 copy.11
  107.3 0.0 all-gather.6.cloned.1.call-update
  107.3 0.0 all-gather.4.cloned.1.call-start
  107.3 29.4 %all_to_all.39 = bf16[128,4,1536]{0,2,1:T(8,128)(2,1)S(1)} all-to-all(bf16[128,4,1536]{0,2,1:T(8,128)(2,1)S(1)} %bitcast.16), channel_id=1, replica_groups=mesh['rep'=4,'row'=4,'col'=8] {'row'}, dimensions={1} | all-to-all | bytes 3145728 | tf_op jit(solution)/shard_map/all_to_all | solution.py:10
  136.7 1.6 copy.10
  138.3 0.0 all-gather.4.cloned.1.call-update
  138.3 0.0 reduce-scatter.5.cloned.1.call-start
  138.4 44.5 %all-gather.6.cloned.1.call-done = bf16[4096,768]{1,0:T(8,128)(2,1)} async-done(((bf16[1024,768]{1,0:T(8,128)(2,1)}), bf16[4096,768]{1,0:T(8,128)(2,1)}) %all-gather.6.cloned.1.call-update) | async-done | bytes 6291472 | tf_op jit(solution)/shard_map/all_gather | solution.py:15
  182.9 6.0 %copy.12 = bf16[4,8,128,768]{3,2,0,1:T(8,128)(2,1)} copy(bf16[4,8,128,768]{3,2,1,0:T(8,128)(2,1)} %bitcast.18) | data formatting | bytes 12582912 | tf_op jit(solution)/shard_map/reshape | solution.py:17
  188.9 123.7 %all-gather.4.cloned.1.call-done = bf16[4096,1536]{1,0:T(8,128)(2,1)} async-done(((bf16[512,1536]{1,0:T(8,128)(2,1)}), bf16[4096,1536]{1,0:T(8,128)(2,1)}) %all-gather.4.cloned.1.call-update) | async-done | bytes 12582928 | tf_op jit(solution)/shard_map/all_gather | solution.py:22
  312.6 16.4 %fusion = f32[1536,768]{1,0:T(8,128)} fusion(bf16[4096,1536]{1,0:T(8,128)(2,1)} %all-gather.4.cloned.1.call-done, bf16[4096,768]{1,0:T(8,128)(2,1)} %bitcast.19), kind=kOutput, calls=%fused_computation.1 | convolution fusion | flops 9663676416 | bytes 23592960 | tf_op jit(solution)/shard_map/dot_general | solution.py:21
  328.9 0.0 reduce-scatter.5.cloned.1.call-update
  328.9 0.0 all-gather.8.cloned.1.call-start
  329.0 53.8 %reduce-scatter.5.cloned.1.call-done = f32[384,768]{1,0:T(8,128)} async-done(((f32[1536,768]{1,0:T(8,128)}), f32[384,768]{1,0:T(8,128)}) %reduce-scatter.5.cloned.1.call-update) | async-done | bytes 1179664 | tf_op jit(solution)/shard_map/reduce_scatter | solution.py:27
  382.8 0.0 all-gather.8.cloned.1.call-update
  382.8 42.9 %all-gather.8.cloned.1.call-done = f32[1536,768]{1,0:T(8,128)} async-done(((f32[384,768]{1,0:T(8,128)}), f32[1536,768]{1,0:T(8,128)}) %all-gather.8.cloned.1.call-update) | async-done | bytes 4718608 | tf_op jit(solution)/shard_map/all_gather | solution.py:28
  425.7 6.8 %multiply_add_fusion = f32[1536,768]{1,0:T(8,128)} fusion(f32[1536,768]{1,0:T(8,128)} %all-gather.8.cloned.1.call-done, f32[1536,768]{1,0:T(8,128)} %param.3), kind=kLoop, calls=%fused_computation | loop fusion | flops 3538944 | bytes 14155776 | tf_op jit(solution)/shard_map/add | solution.py:29
  432.6 2.2 copy.17
  (2 shorter events, 0.0 us)
Async XLA Ops:
  7.2 72.4 %reduce-scatter.7.cloned.1.call-start = ((), (), s32[]{:S(2)}) async-start(), calls=%async_computation.8 | async-start | bytes 7864320
  7.9 175.0 %all-gather.6.cloned.1.call-start = ((), (), s32[]{:S(2)}) async-start(), calls=%async_computation.5 | async-start | bytes 7864320 | tf_op jit(solution)/shard_map/all_gather | solution.py:15
  107.3 205.3 %all-gather.4.cloned.1.call-start = ((), (), s32[]{:S(2)}) async-start(), calls=%async_computation.4 | async-start | bytes 14155776 | tf_op jit(solution)/shard_map/all_gather | solution.py:22
  138.3 244.5 %reduce-scatter.5.cloned.1.call-start = ((), (), s32[]{:S(2)}) async-start(), calls=%async_computation.6 | async-start | bytes 5898240 | tf_op jit(solution)/shard_map/reduce_scatter | solution.py:27
  328.9 96.8 %all-gather.8.cloned.1.call-start = ((), (), s32[]{:S(2)}) async-start(), calls=%async_computation.7 | async-start | bytes 5898240 | tf_op jit(solution)/shard_map/all_gather | solution.py:28
  425.7 6.9 %copy-start = (f32[1536,768]{1,0:T(8,128)S(1)}, f32[1536,768]{1,0:T(8,128)}, u32[]{:S(2)}) copy-start(f32[1536,768]{1,0:T(8,128)} %all-gather.8.cloned.1.call-done) | copy-start | bytes 14155780
Sparse Core Ops, SparseCore 0:
  10.6 68.9 reduce-scatter.6
  107.4 75.4 all-gather.5
  185.1 127.4 all-gather.3
  329.1 53.6 reduce-scatter.4
  384.3 41.3 all-gather.7
where the time goes:
time: 442 us; the launch traced here: 441 us
  waiting for transfers between devices  337 us (76%)
  blocking collectives  53.6 us (12%)
  matrix products  16.4 us (4%)
  between operations  13.8 us (3%)
  local copies, waits for them, and re-layouts  13.3 us (3%)
  other arithmetic  6.85 us (2%)
    all_gather x1, waiting for transfers between devices, shards(): lax.all_gather(rows_panel, 'col', axis=0, tiled=True)  124 us
    unnamed x6, waiting for transfers between devices  72.4 us
    reduce_scatter x1, waiting for transfers between devices, shards(): lax.psum_scatter(partial_tile, 'rep', scatter_dimension=0, tiled=True)  53.8 us
    all_gather x1, waiting for transfers between devices, shards(): right_whole = lax.all_gather(cols_panel, 'row', axis=0, tiled=True)  44.5 us
    all_gather x1, waiting for transfers between devices, shards(): gram_tile = lax.all_gather(portion, 'rep', axis=0, tiled=True)  42.9 us
    all_to_all x1, blocking collectives, shards(): lax.all_to_all(summed, 'row', split_axis=1, concat_axis=0, tiled=True)  29.4 us
    all_to_all x1, blocking collectives, shards(): lax.all_to_all(summed, 'col', split_axis=1, concat_axis=0, tiled=True)  24.2 us
    dot_general x1, matrix products, shards(): lax.dot_general(lax.all_gather(rows_panel, 'col', axis=0, tiled=True), ri...  16.4 us
  transfers between devices with their start and end apart: 5, of which 5 were waited for; matrix products, arithmetic and copies ran while one was open for 2% of the time, Pallas kernels for 0%

commit v1 on v0

--- a/solution.py
+++ b/solution.py
@@ -1,7 +1,40 @@
+import functools
 import jax
 import jax.numpy as jnp
 from jax import lax
 from jax.sharding import PartitionSpec as P
+from jax.lax import axis_index, axis_size, ppermute
+
+
+def answer_the_body(panel, axis_no):
+    then = axis_size("row")
+    even, carry, ready = (then, axis_index("row"), panel.shape[axis_no])
+    pieces_in = []
+    for no in tuple(range(even)):
+        pieces_in.append((no, (no + 1) % even))
+    copies = []
+    for no in [*range(even)]:
+        copies.append((no, (no - 1) % even))
+    x_next = jnp.zeros(
+        (*panel.shape[:axis_no], even * ready, *panel.shape[axis_no + 1 :]), panel.dtype
+    )
+    x_next = lax.dynamic_update_slice_in_dim(x_next, panel, carry * ready, axis=axis_no)
+    y_new = e_next = panel
+    right_arr = even // 2
+    for ix in [*range(1, right_arr + 1)]:
+        y_new = ppermute(y_new, "row", pieces_in)
+        x_next = lax.dynamic_update_slice_in_dim(
+            x_next, y_new, (carry - ix) % even * ready, axis=axis_no
+        )
+        if ix < even - right_arr:
+            e_next = ppermute(e_next, "row", copies)
+            x_next = lax.dynamic_update_slice_in_dim(
+                x_next, e_next, (carry + ix) % even * ready, axis=axis_no
+            )
+    return x_next
+
+
+wait_row = functools.partial(answer_the_body, axis_no=0)
 
 
 def shards(grad_parts, statistic):
@@ -12,7 +45,7 @@
     row_count = lax.axis_size("row")
     col_count = lax.axis_size("col")
     quarter = summed.shape[0]
-    right_whole = lax.all_gather(cols_panel, "row", axis=0, tiled=True)
+    right_whole = wait_row(cols_panel)
     right_order = (
         right_whole.reshape(row_count, col_count, quarter, -1)
         .transpose(1, 0, 2, 3)

time: 442 us -> 387 us (0.88)
  waiting for transfers between devices: 337 us -> 262 us
  local copies, waits for them, and re-layouts: 13.3 us -> 29.2 us
    all_gather x1, waiting for transfers between devices: 124 us -> 46.6 us  [shards(): lax.all_gather(rows_panel, 'col', axis=0, tiled=True)]
    ppermute x0 -> x3, waiting for transfers between devices: none -> 55.7 us  [the longest x2 55.7 us: answer_the_body(): y_new = ppermute(y_new, 'row', pieces_in)]
    all_gather x1 -> x0, waiting for transfers between devices: 44.5 us -> none  [shards(): right_whole = lax.all_gather(cols_panel, 'row', axis=0, tiled=True)]
    unnamed x4, local copies, waits for them, and re-layouts: 4.1 us -> 20 us
    all_to_all x1, blocking collectives: 24.2 us -> 31.5 us  [shards(): lax.all_to_all(summed, 'col', split_axis=1, concat_axis=0, tiled=True)]
    all_gather x1, waiting for transfers between devices: 42.9 us -> 36.9 us  [shards(): gram_tile = lax.all_gather(portion, 'rep', axis=0, tiled=True)]
    reshape x1 -> x0, local copies, waits for them, and re-layouts: 6.04 us -> none  [shards(): right_whole.reshape(row_count, col_count, quarter, -1).transpose(1, 0, 2, 3)]
    all_to_all x1, blocking collectives: 29.4 us -> 23.5 us  [shards(): lax.all_to_all(summed, 'row', split_axis=1, concat_axis=0, tiled=True)]
  transfers between devices with their start and end apart: 5 -> 7, of which waited for: 5 -> 6; matrix products, arithmetic and copies ran while one was open for 2% -> 4% of each run, Pallas kernels for 0% -> 0%
where the time goes in v1:
time: 387 us; the launch traced here: 386 us
  waiting for transfers between devices  262 us (68%)
  blocking collectives  55 us (14%)
  local copies, waits for them, and re-layouts  29.2 us (8%)
  matrix products  16.3 us (4%)
  between operations  13.8 us (4%)
  other arithmetic  7.07 us (2%)
    unnamed x5, waiting for transfers between devices  72.4 us
    ppermute x2, waiting for transfers between devices, answer_the_body(): y_new = ppermute(y_new, 'row', pieces_in)  55.7 us
    reduce_scatter x1, waiting for transfers between devices, shards(): lax.psum_scatter(partial_tile, 'rep', scatter_dimension=0, tiled=True)  50.4 us
    all_gather x1, waiting for transfers between devices, shards(): lax.all_gather(rows_panel, 'col', axis=0, tiled=True)  46.6 us
    all_gather x1, waiting for transfers between devices, shards(): gram_tile = lax.all_gather(portion, 'rep', axis=0, tiled=True)  36.9 us
    all_to_all x1, blocking collectives, shards(): lax.all_to_all(summed, 'col', split_axis=1, concat_axis=0, tiled=True)  31.5 us
    all_to_all x1, blocking collectives, shards(): lax.all_to_all(summed, 'row', split_axis=1, concat_axis=0, tiled=True)  23.5 us
    unnamed x4, local copies, waits for them, and re-layouts  20 us
  transfers between devices with their start and end apart: 7, of which 6 were waited for; matrix products, arithmetic and copies ran while one was open for 4% of the time, Pallas kernels for 0%

profile of v1, /device:TPU:1, one launch (start us, length us, event | category | flops | bytes accessed | tf_op | source)
XLA Modules:
  0.0 386.2 jit_solution(13348658719325743367)
XLA Ops:
  7.2 0.7 reduce-scatter.7.cloned.1.call-update
  7.9 71.7 %reduce-scatter.7.cloned.1.call-done = bf16[128,6144]{1,0:T(8,128)(2,1)} async-done(((bf16[512,6144]{1,0:T(8,128)(2,1)}), bf16[128,6144]{1,0:T(8,128)(2,1)}) %reduce-scatter.7.cloned.1.call-update) | async-done | bytes 1572880
  79.6 1.9 copy.25
  81.5 23.5 %all_to_all.38 = bf16[128,4,1536]{0,2,1:T(8,128)(2,1)S(1)} all-to-all(bf16[128,4,1536]{0,2,1:T(8,128)(2,1)S(1)} %bitcast.18), channel_id=1, replica_groups=mesh['rep'=4,'row'=4,'col'=8] {'row'}, dimensions={1} | all-to-all | bytes 3145728 | tf_op jit(solution)/shard_map/all_to_all | solution.py:43
  105.0 1.6 copy.20
  106.6 31.5 %all_to_all.39 = bf16[128,8,768]{0,2,1:T(8,128)(2,1)S(1)} all-to-all(bf16[128,8,768]{0,2,1:T(8,128)(2,1)S(1)} %bitcast.19), channel_id=1, replica_groups=mesh['rep'=4,'row'=4,'col'=8] {'col'}, dimensions={1} | all-to-all | bytes 3145728 | tf_op jit(solution)/shard_map/all_to_all | solution.py:44
  138.1 0.7 copy.18
  138.9 2.7 collective-permute-start.1
  141.6 25.1 %collective-permute-done = bf16[1024,768]{1,0:T(8,128)(2,1)S(1)} collective-permute-done((bf16[1024,768]{1,0:T(8,128)(2,1)S(1)}, bf16[1024,768]{1,0:T(8,128)(2,1)S(1)}, u32[]{:S(2)}, u32[]{:S(2)}) %collective-permute-start) | collective-permute-done | bytes 1572896 | tf_op jit(solution)/shard_map/ppermute | solution.py:25
  166.6 0.4 broadcast_in_dim.3
  167.1 0.2 constant_dynamic-update-slice_fusion.3
  167.2 0.2 constant_dynamic-update-slice_fusion.2
  167.4 1.6 constant_dynamic-update-slice_fusion.1
  169.0 30.6 %collective-permute-done.2 = bf16[1024,768]{1,0:T(8,128)(2,1)} collective-permute-done((bf16[1024,768]{1,0:T(8,128)(2,1)S(1)}, bf16[1024,768]{1,0:T(8,128)(2,1)}, u32[]{:S(2)}, u32[]{:S(2)}) %collective-permute-start.2) | collective-permute-done | bytes 1572896 | tf_op jit(solution)/shard_map/ppermute | solution.py:25
  199.6 1.6 constant_dynamic-update-slice_fusion
  201.2 3.0 copy.19
  204.2 46.6 %all-gather.3.cloned.1.call-done = bf16[4096,1536]{1,0:T(8,128)(2,1)} async-done(((bf16[512,1536]{1,0:T(8,128)(2,1)}), bf16[4096,1536]{1,0:T(8,128)(2,1)}) %all-gather.3.cloned.1.call-update) | async-done | bytes 12582928 | tf_op jit(solution)/shard_map/all_gather | solution.py:55
  250.8 16.3 %convolution_bitcast_fusion = f32[1536,768]{0,1:T(8,128)} fusion(bf16[4096,768]{1,0:T(8,128)(2,1)} %bitcast.21, bf16[4096,1536]{1,0:T(8,128)(2,1)} %all-gather.3.cloned.1.call-done), kind=kOutput, calls=%fused_computation.1 | convolution fusion | flops 9663676416 | bytes 23592960 | tf_op jit(solution)/shard_map/dot_general | solution.py:54
  267.2 50.4 %reduce-scatter.5.cloned.1.call-done = f32[384,768]{0,1:T(8,128)} async-done(((f32[1536,768]{0,1:T(8,128)}), f32[384,768]{0,1:T(8,128)}) %reduce-scatter.5.cloned.1.call-update) | async-done | bytes 1179664 | tf_op jit(solution)/shard_map/reduce_scatter | solution.py:60
  317.6 6.0 %copy.21 = f32[1536,768]{0,1:T(8,128)} copy(f32[1536,768]{1,0:T(8,128)} %param.3) | data formatting | bytes 9437184 | tf_op args[1]
  323.7 36.9 %all-gather.5.cloned.1.call-done = f32[1536,768]{0,1:T(8,128)} async-done(((f32[384,768]{0,1:T(8,128)}), f32[1536,768]{0,1:T(8,128)}) %all-gather.5.cloned.1.call-update) | async-done | bytes 4718608 | tf_op jit(solution)/shard_map/all_gather | solution.py:61
  360.5 7.1 %multiply_add_fusion = f32[1536,768]{0,1:T(8,128)} fusion(f32[1536,768]{0,1:T(8,128)} %all-gather.5.cloned.1.call-done, f32[1536,768]{0,1:T(8,128)} %copy.21), kind=kLoop, calls=%fused_computation | loop fusion | flops 3538944 | bytes 14155776 | tf_op jit(solution)/shard_map/add | solution.py:62
  367.6 6.0 %copy.23 = f32[1536,768]{1,0:T(8,128)} copy(f32[1536,768]{0,1:T(8,128)} %multiply_add_fusion) | data formatting | bytes 9437184
  373.6 6.0 %copy.22 = f32[1536,768]{1,0:T(8,128)} copy(f32[1536,768]{0,1:T(8,128)} %all-gather.5.cloned.1.call-done) | data formatting | bytes 9437184
  (10 shorter events, 0.3 us)
Async XLA Ops:
  7.2 72.4 %reduce-scatter.7.cloned.1.call-start = ((), (), s32[]{:S(2)}) async-start(), calls=%async_computation.7 | async-start | bytes 7864320
  7.9 242.9 %all-gather.3.cloned.1.call-start = ((), (), s32[]{:S(2)}) async-start(), calls=%async_computation.4 | async-start | bytes 14155776 | tf_op jit(solution)/shard_map/all_gather | solution.py:55
  106.5 211.0 %reduce-scatter.5.cloned.1.call-start = ((), (), s32[]{:S(2)}) async-start(), calls=%async_computation.5 | async-start | bytes 5898240 | tf_op jit(solution)/shard_map/reduce_scatter | solution.py:60
  138.8 27.8 %collective-permute-start = (bf16[1024,768]{1,0:T(8,128)(2,1)S(1)}, bf16[1024,768]{1,0:T(8,128)(2,1)S(1)}, u32[]{:S(2)}, u32[]{:S(2)}) collective-permute-start(bf16[1024,768]{1,0:T(8,128)(2,1)S(1)} %bitcast.25), channel_id=1, source_target_pairs={{0,8},{8,16},{16,24},{24,0},{1,9},{9,17},{17,25},{25,1},{2,10},{10... | collective-permute-start | bytes 4718600 | tf_op jit(solution)/shard_map/ppermute | solution.py:25
  138.9 28.5 %collective-permute-start.1 = (bf16[1024,768]{1,0:T(8,128)(2,1)S(1)}, bf16[1024,768]{1,0:T(8,128)(2,1)}, u32[]{:S(2)}, u32[]{:S(2)}) collective-permute-start(bf16[1024,768]{1,0:T(8,128)(2,1)S(1)} %bitcast.26), channel_id=1, source_target_pairs={{0,24},{8,0},{16,8},{24,16},{1,25},{9,1},{17,9},{25,17},{2,26},{10... | collective-permute-start | bytes 4718600 | tf_op jit(solution)/shard_map/ppermute | solution.py:30
  166.6 33.0 %collective-permute-start.2 = (bf16[1024,768]{1,0:T(8,128)(2,1)S(1)}, bf16[1024,768]{1,0:T(8,128)(2,1)}, u32[]{:S(2)}, u32[]{:S(2)}) collective-permute-start(bf16[1024,768]{1,0:T(8,128)(2,1)S(1)} %collective-permute-done), channel_id=1, source_target_pairs={{0,8},{8,16},{16,24},{24,0},{1,9},{9,17},{17,25},{25,1},{2,10},{10... | collective-permute-start | bytes 4718600 | tf_op jit(solution)/shard_map/ppermute | solution.py:25
  267.1 93.4 %all-gather.5.cloned.1.call-start = ((), (), s32[]{:S(2)}) async-start(), calls=%async_computation.6 | async-start | bytes 5898240 | tf_op jit(solution)/shard_map/all_gather | solution.py:61
Sparse Core Ops, SparseCore 0:
  10.6 68.9 reduce-scatter.6
  106.7 144.1 all-gather.2
  267.3 50.2 reduce-scatter.4
  319.1 41.3 all-gather.4

commit v2 on v0

--- a/solution.py
+++ b/solution.py
@@ -7,7 +7,9 @@
 def shards(grad_parts, statistic):
     own_part = grad_parts[0].astype(jnp.float32)
     summed = lax.psum_scatter(own_part.astype(jnp.bfloat16), "rep", scatter_dimension=0, tiled=True)
-    rows_panel = lax.all_to_all(summed, "row", split_axis=1, concat_axis=0, tiled=True)
+    pieces = jnp.split(summed, lax.axis_size("row"), axis=1)
+    received = lax.all_to_all(jnp.stack(pieces), "row", 0, 0)
+    rows_panel = jnp.concatenate(received, axis=0)
     cols_panel = lax.all_to_all(summed, "col", split_axis=1, concat_axis=0, tiled=True)
     row_count = lax.axis_size("row")
     col_count = lax.axis_size("col")

time: 442 us -> 442 us (level)
    reduce_scatter x0 -> x1, waiting for transfers between devices: none -> 71.7 us  [shards(): lax.psum_scatter(own_part.astype(jnp.bfloat16), 'rep', scatter_dimension=...]
    unnamed x6 -> x5, waiting for transfers between devices: 72.4 us -> 0.75 us
  transfers between devices with their start and end apart: 5 -> 5, of which waited for: 5 -> 5; matrix products, arithmetic and copies ran while one was open for 2% -> 1% of each run, Pallas kernels for 0% -> 0%
where the time goes in v2:
time: 442 us
  waiting for transfers between devices  338 us (76%)
  blocking collectives  54.3 us (12%)
  matrix products  16.4 us (4%)
  between operations  13.8 us (3%)
  local copies, waits for them, and re-layouts  12.5 us (3%)
  other arithmetic  7.05 us (2%)
    all_gather x1, waiting for transfers between devices, shards(): lax.all_gather(rows_panel, 'col', axis=0, tiled=True)  123 us
    reduce_scatter x1, waiting for transfers between devices, shards(): lax.psum_scatter(own_part.astype(jnp.bfloat16), 'rep', scatter_dimension=...  71.7 us
    reduce_scatter x1, waiting for transfers between devices, shards(): lax.psum_scatter(partial_tile, 'rep', scatter_dimension=0, tiled=True)  53.8 us
    all_gather x1, waiting for transfers between devices, shards(): right_whole = lax.all_gather(cols_panel, 'row', axis=0, tiled=True)  45.7 us
    all_gather x1, waiting for transfers between devices, shards(): gram_tile = lax.all_gather(portion, 'rep', axis=0, tiled=True)  42.9 us
    all_to_all x1, blocking collectives, shards(): received = lax.all_to_all(jnp.stack(pieces), 'row', 0, 0)  29.8 us
    all_to_all x1, blocking collectives, shards(): lax.all_to_all(summed, 'col', split_axis=1, concat_axis=0, tiled=True)  24.5 us
    dot_general x1, matrix products, shards(): lax.dot_general(lax.all_gather(rows_panel, 'col', axis=0, tiled=True), ri...  16.4 us
  transfers between devices with their start and end apart: 5, of which 5 were waited for; matrix products, arithmetic and copies ran while one was open for 1% of the time, Pallas kernels for 0%

profile of v2, /device:TPU:1, one launch (start us, length us, event | category | flops | bytes accessed | tf_op | source)
XLA Modules:
  0.0 442.1 jit_solution(6368349544627946037)
XLA Ops:
  7.2 0.0 reduce-scatter.3.cloned.1.call-start
  7.2 0.7 reduce-scatter.3.cloned.1.call-update
  7.9 0.0 all-gather.6.cloned.1.call-start
  7.9 71.7 %reduce-scatter.3.cloned.1.call-done = bf16[128,6144]{1,0:T(8,128)(2,1)} async-done(((bf16[512,6144]{1,0:T(8,128)(2,1)}), bf16[128,6144]{1,0:T(8,128)(2,1)}) %reduce-scatter.3.cloned.1.call-update) | async-done | bytes 1572880 | tf_op jit(solution)/shard_map/reduce_scatter | solution.py:9
  79.6 2.6 copy.8
  82.2 24.5 %all_to_all.24 = bf16[128,8,768]{0,2,1:T(8,128)(2,1)S(1)} all-to-all(bf16[128,8,768]{0,2,1:T(8,128)(2,1)} %bitcast.25), channel_id=1, replica_groups=mesh['rep'=4,'row'=4,'col'=8] {'col'}, dimensions={1} | all-to-all | bytes 3145728 | tf_op jit(solution)/shard_map/all_to_all | solution.py:13
  106.7 1.6 copy.9
  108.2 0.0 all-gather.6.cloned.1.call-update
  108.3 0.0 all-gather.4.cloned.1.call-start
  108.3 0.1 slice_bitcast_fusion.3
  108.5 0.2 pad_maximum_fusion
  108.7 29.8 %all_to_all.25 = bf16[4,128,1536]{2,1,0:T(8,128)(2,1)} all-to-all(bf16[4,128,1536]{2,1,0:T(8,128)(2,1)S(1)} %pad_maximum_fusion), channel_id=1, replica_groups=mesh['rep'=4,'row'=4,'col'=8] {'row'}, dimensions={0} | all-to-all | bytes 3145728 | tf_op jit(solution)/shard_map/all_to_all | solution.py:11
  138.4 0.0 all-gather.4.cloned.1.call-update
  138.5 0.0 reduce-scatter.5.cloned.1.call-start
  138.5 45.7 %all-gather.6.cloned.1.call-done = bf16[4096,768]{1,0:T(8,128)(2,1)} async-done(((bf16[1024,768]{1,0:T(8,128)(2,1)}), bf16[4096,768]{1,0:T(8,128)(2,1)}) %all-gather.6.cloned.1.call-update) | async-done | bytes 6291472 | tf_op jit(solution)/shard_map/all_gather | solution.py:17
  184.2 6.0 %copy.10 = bf16[4,8,128,768]{3,2,0,1:T(8,128)(2,1)} copy(bf16[4,8,128,768]{3,2,1,0:T(8,128)(2,1)} %bitcast.20) | data formatting | bytes 12582912 | tf_op jit(solution)/shard_map/reshape | solution.py:19
  190.2 123.1 %all-gather.4.cloned.1.call-done = bf16[4096,1536]{1,0:T(8,128)(2,1)} async-done(((bf16[512,1536]{1,0:T(8,128)(2,1)}), bf16[4096,1536]{1,0:T(8,128)(2,1)}) %all-gather.4.cloned.1.call-update) | async-done | bytes 12582928 | tf_op jit(solution)/shard_map/all_gather | solution.py:24
  313.3 16.4 %fusion = f32[1536,768]{1,0:T(8,128)} fusion(bf16[4096,1536]{1,0:T(8,128)(2,1)} %all-gather.4.cloned.1.call-done, bf16[4096,768]{1,0:T(8,128)(2,1)} %bitcast.21), kind=kOutput, calls=%fused_computation.6 | convolution fusion | flops 9663676416 | bytes 23592960 | tf_op jit(solution)/shard_map/dot_general | solution.py:23
  329.7 0.0 all-gather.8.cloned.1.call-start
  329.7 53.8 %reduce-scatter.5.cloned.1.call-done = f32[384,768]{1,0:T(8,128)} async-done(((f32[1536,768]{1,0:T(8,128)}), f32[384,768]{1,0:T(8,128)}) %reduce-scatter.5.cloned.1.call-update) | async-done | bytes 1179664 | tf_op jit(solution)/shard_map/reduce_scatter | solution.py:29
  383.6 0.0 all-gather.8.cloned.1.call-update
  383.6 42.9 %all-gather.8.cloned.1.call-done = f32[1536,768]{1,0:T(8,128)} async-done(((f32[384,768]{1,0:T(8,128)}), f32[1536,768]{1,0:T(8,128)}) %all-gather.8.cloned.1.call-update) | async-done | bytes 4718608 | tf_op jit(solution)/shard_map/all_gather | solution.py:30
  426.5 6.8 %multiply_add_fusion = f32[1536,768]{1,0:T(8,128)} fusion(f32[1536,768]{1,0:T(8,128)} %all-gather.8.cloned.1.call-done, f32[1536,768]{1,0:T(8,128)} %param.3), kind=kLoop, calls=%fused_computation | loop fusion | flops 3538944 | bytes 14155776 | tf_op jit(solution)/shard_map/add | solution.py:31
  433.4 2.2 copy.12
  (5 shorter events, 0.0 us)
Async XLA Ops:
  7.2 72.4 %reduce-scatter.3.cloned.1.call-start = ((), (), s32[]{:S(2)}) async-start(), calls=%async_computation.4 | async-start | bytes 7864320 | tf_op jit(solution)/shard_map/reduce_scatter | solution.py:9
  7.9 176.3 %all-gather.6.cloned.1.call-start = ((), (), s32[]{:S(2)}) async-start(), calls=%async_computation.6 | async-start | bytes 7864320 | tf_op jit(solution)/shard_map/all_gather | solution.py:17
  82.2 26.2 %copy-start.1 = (bf16[128,6144]{1,0:T(8,128)(2,1)S(1)}, bf16[128,6144]{1,0:T(8,128)(2,1)}, u32[]{:S(2)}) copy-start(bf16[128,6144]{1,0:T(8,128)(2,1)} %reduce-scatter.3.cloned.1.call-done) | copy-start | bytes 4718596
  108.3 205.1 %all-gather.4.cloned.1.call-start = ((), (), s32[]{:S(2)}) async-start(), calls=%async_computation.5 | async-start | bytes 14155776 | tf_op jit(solution)/shard_map/all_gather | solution.py:24
  138.5 245.1 %reduce-scatter.5.cloned.1.call-start = ((), (), s32[]{:S(2)}) async-start(), calls=%async_computation.7 | async-start | bytes 5898240 | tf_op jit(solution)/shard_map/reduce_scatter | solution.py:29
  329.7 96.8 %all-gather.8.cloned.1.call-start = ((), (), s32[]{:S(2)}) async-start(), calls=%async_computation.8 | async-start | bytes 5898240 | tf_op jit(solution)/shard_map/all_gather | solution.py:30
  426.5 6.9 %copy-start = (f32[1536,768]{1,0:T(8,128)S(1)}, f32[1536,768]{1,0:T(8,128)}, u32[]{:S(2)}) copy-start(f32[1536,768]{1,0:T(8,128)} %all-gather.8.cloned.1.call-done) | copy-start | bytes 14155780
Sparse Core Ops, SparseCore 0:
  10.6 68.9 reduce-scatter.2
  108.4 75.7 all-gather.5
  185.9 127.4 all-gather.3
  329.8 53.6 reduce-scatter.4
  385.1 41.3 all-gather.7
